TPU v7x, 32 devices: a whole 2x2x4 slice. The times are simulated.
32 devices in a mesh: wa: 8 (over z, x), ga: 4 (over y, core).
Axes of the slice: x: 2, y: 2, z: 4, core: 2. Of those that a mesh axis runs over, the one named last changes fastest.
Arguments:
- plane_ids: int32 [192], P(('ga', 'wa')), may hold values from 0 to 191, each once
- weighting: float32 [192, 256, 256], P(('ga', 'wa')), may hold values from -5 to 5
Outputs:
- kernel_table: bfloat16 [192, 64, 2048], P(None, 'wa')
Inputs may be any that keep to these rules, and one draw needn't show every extreme that they name: `plane_ids`: every plane number appears in exactly one slot.
All inputs are finite; a program needn't handle non-finite values.
Results may differ from a plain program's by a relative error of at most 0.003.
Values may be sent and summed in bfloat16 or wider, within the bound.
A program may use at most 64 MiB of HBM per device.

v0:
```python
import functools
import math

import jax
import jax.numpy as jnp
import numpy as np
from jax import lax
from jax.experimental import pallas as pl
from jax.experimental.pallas import tpu as pltpu
from jax.sharding import PartitionSpec as P

OS = 8
S = 32
RANK = 64
LANES = 128

field_width = 0.2
w_top = 2000.0


def split(x):
    hi = x.astype(jnp.bfloat16)
    lo = (x - hi.astype(jnp.float32)).astype(jnp.bfloat16)
    return hi, lo


def np_split(x):
    hi = np.asarray(x, np.float32).astype(jnp.bfloat16)
    lo = (x - hi.astype(np.float64)).astype(np.float32).astype(jnp.bfloat16)
    return hi, lo


@functools.lru_cache(None)
def factors(pixels):
    x = np.arange(pixels) - pixels // 2
    rows = np.arange(OS * S)
    u = (rows % S - S // 2) * OS + rows // S
    period = pixels * OS
    f = np.exp(-2j * np.pi * (u[:, None] * x[None, :] % period) / period)
    half = np.exp(1j * np.pi * x / period)
    centred = f / half[None, :]
    _, _, vh = np.linalg.svd(np.concatenate([centred.real, centred.imag], 0), full_matrices=False)
    v = vh[:RANK].T
    p = centred @ v
    return v, p.real, p.imag


def tables(pixels):
    v, pr, pi = factors(pixels)
    zero = np.zeros_like(v)
    q_re = np_split(np.concatenate([v, zero], 1))
    q_im = np_split(np.concatenate([zero, v], 1))
    vt = np_split(v.T)
    order = np.arange(OS * S).reshape(OS, S // 4, 4).transpose(0, 2, 1).reshape(-1)
    left = np_split(np.concatenate([pr, pi], 1)[order] / pixels)
    right = np.concatenate(
        [np.concatenate([pr.T, pi.T], 1), np.concatenate([-pi.T, pr.T], 1)], 0
    )
    coord = (np.arange(pixels) - pixels // 2) / pixels * field_width
    radius = coord[:, None] ** 2 + coord[None, :] ** 2
    nterm = (-radius / (1.0 + np.sqrt(1.0 - radius))).astype(np.float32)
    return q_re + q_im + vt + left, np_split(right), nterm


def dot3(a, b):
    def dot(x, y):
        return jnp.dot(x, y, preferred_element_type=jnp.float32)

    return dot(a[0], b[0]) + dot(a[0], b[1]) + dot(a[1], b[0])


def half_kernel(
    total, planes, weight, nterm, qrh, qrl, qih, qil, vth, vtl, lh, ll, out, grh, grl, gih, gil
):
    pixels = weight.shape[1]
    step = 32
    wvalue = w_top * planes[pl.program_id(0)].astype(jnp.float32) / total

    @pl.loop(0, pixels // step)
    def _(chunk):
        start = pl.multiple_of(chunk * step, step)
        rows = pl.ds(start, step)
        iota = lambda d: lax.broadcasted_iota(jnp.int32, (step, pixels), d)
        shift = (iota(0) + iota(1) + (start - pixels)).astype(jnp.float32) / (2 * pixels * OS)
        turns = wvalue * nterm[rows, :]
        frac = turns - jnp.round(turns) - shift
        frac = frac - jnp.round(frac)
        y = math.pi * frac
        z = y * y
        s = jnp.full_like(z, -1.0 / math.factorial(11))
        for k in (9, 7, 5, 3, 1):
            s = s * z + (-1.0) ** (k // 2) / math.factorial(k)
        s = s * y
        c = jnp.full_like(z, 1.0 / math.factorial(12))
        for k in (10, 8, 6, 4, 2, 0):
            c = c * z + (-1.0) ** (k // 2) / math.factorial(k)
        w = weight[0, rows, :]
        g_re = w * (1.0 - 2.0 * s * s)
        g_im = w * (-2.0 * s * c)
        grh[rows, :], grl[rows, :] = split(g_re)
        gih[rows, :], gil[rows, :] = split(g_im)

    t = dot3((grh[...], grl[...]), (qrh[...], qrl[...]))
    t += dot3((gih[...], gil[...]), (qih[...], qil[...]))
    core = dot3((vth[...], vtl[...]), split(t))
    lane = lax.broadcasted_iota(jnp.int32, core.shape, 1)
    turned = pltpu.roll(core, RANK, 1)
    turned = jnp.where(lane < RANK, -turned, turned)
    stacked = jnp.concatenate([core, turned], 0)
    a = dot3((lh[...], ll[...]), split(stacked))
    out[...] = a.reshape(out.shape)


def half_transform(plane_ids, weighting, total, small, nterm):
    slots, pixels = weighting.shape[:2]
    whole = lambda a: pl.BlockSpec(a.shape, lambda s, p: (0,) * a.ndim)
    args = (nterm,) + small
    return pl.pallas_call(
        functools.partial(half_kernel, total),
        grid_spec=pltpu.PrefetchScalarGridSpec(
            num_scalar_prefetch=1,
            grid=(slots,),
            in_specs=[pl.BlockSpec((1, pixels, pixels), lambda s, p: (s, 0, 0))]
            + [whole(a) for a in args],
            out_specs=pl.BlockSpec((OS, 1, S, LANES), lambda s, p: (0, s, 0, 0)),
            scratch_shapes=[pltpu.VMEM((pixels, pixels), jnp.bfloat16)] * 4,
        ),
        out_shape=jax.ShapeDtypeStruct((OS, slots, S, LANES), jnp.float32),
        name="half_transform",
    )(plane_ids, weighting, *args)


def expand_kernel(kept, x, th, tl, out, full, mixed):
    count = x.shape[0]
    group = 2
    flat = x[...].reshape(count * S, LANES)
    full[...] = dot3(split(flat), (th[...], tl[...])).reshape(full.shape)
    lane = lax.broadcasted_iota(jnp.int32, (group * 8, LANES), 1) // S

    @pl.loop(0, count // group)
    def _(i):
        slots = pl.ds(i * group, group)
        for comp in range(2):
            for half in range(2):
                tile = comp * 2 + half
                cols = slice(tile * LANES, (tile + 1) * LANES)
                src = [
                    full[slots, c * 8 : (c + 1) * 8, cols].reshape(group * 8, LANES)
                    for c in range(4)
                ]
                src = [src[0]] + [pltpu.roll(src[c], S * c, 1) for c in range(1, 4)]
                for m in range(4):
                    kr = half * 4 + m
                    if kr >= kept:
                        continue
                    y = src[(3 - m) % 4]
                    for b in range(3):
                        y = jnp.where(lane == b, src[(b - m) % 4], y)
                    if m:
                        y = pltpu.roll(y, LANES - S * m, 1)
                    mixed[slots, comp, pl.ds(kr, 8, stride=kept), :] = y.reshape(group, 8, LANES)
        out[slots] = mixed[slots].reshape(group, 16 * kept, LANES).astype(out.dtype)


def expand(arrived, right, kept, count):
    total = arrived.shape[0]
    whole = lambda a: pl.BlockSpec(a.shape, lambda i: (0,) * a.ndim)
    return pl.pallas_call(
        functools.partial(expand_kernel, kept),
        grid=(total // count,),
        in_specs=[pl.BlockSpec((count, S, LANES), lambda i: (i, 0, 0))] + [whole(a) for a in right],
        out_specs=pl.BlockSpec((count, 16 * kept, LANES), lambda i: (i, 0, 0)),
        out_shape=jax.ShapeDtypeStruct((total, 16 * kept, LANES), jnp.bfloat16),
        scratch_shapes=[
            pltpu.VMEM((count, S, 4 * LANES), jnp.float32),
            pltpu.VMEM((count, 2, 8 * kept, LANES), jnp.float32),
        ],
        name="expand",
    )(arrived, *right)


def regroup(halves):
    moved = lax.all_to_all(halves, "wa", split_axis=0, concat_axis=0, tiled=True)
    return lax.all_gather(moved, "ga", axis=0, tiled=True)


def shards(plane_ids, weighting):
    slots, pixels = weighting.shape[:2]
    wa_count = lax.axis_size("wa")
    ga_count = lax.axis_size("ga")
    total = slots * wa_count * ga_count
    kept = OS * OS // wa_count
    small, right, nterm = tables(pixels)
    halves = half_transform(plane_ids, weighting, total, small, nterm)
    if kept < OS:
        halves = jnp.repeat(halves, OS // kept, axis=0)
        start = lax.axis_index("wa") * kept % OS
        turn = lambda t: jnp.roll(t.reshape(LANES, 2, OS, S), -start, 2).reshape(t.shape)
        right = tuple(turn(jnp.asarray(t)) for t in right)
    arrived = regroup(halves).reshape(total, S, LANES)
    table = expand(arrived, right, kept, 4 * slots)
    table = table.reshape(total, 16, kept, LANES).transpose(0, 2, 1, 3)
    return table.reshape(total, kept, 2 * S * S)


def solution(mesh):
    return jax.shard_map(
        shards,
        mesh=mesh,
        in_specs=(P(("ga", "wa")), P(("ga", "wa"), None, None)),
        out_specs=P(None, "wa", None),
        check_vma=False,
    )
```

profile of v0, /device:TPU:0, one launch (start us, length us, event | category | flops | bytes accessed | tf_op | source)
XLA Modules:
  0.0 104.4 jit_solution(6413572423829662289)
XLA Ops:
  6.5 0.0 all-gather.2.cloned.1.call-start
  6.5 10.7 %half_transform.1 = f32[8,6,32,128]{3,2,1,0:T(8,128)} custom-call(s32[6]{0:T(128)} %planes.1, f32[6,256,256]{2,1,0:T(8,128)} %weight.1, f32[256,256]{1,0:T(8,128)} %constant.22.clone.nterm, bf16[256,128]{1,0:T(8,128)(2,1)} %constant.23.clone.qrh, bf16[256,128]{1,0:T(8,128)(2,1)} %constant.24.clone.qrl, bf16[256,128]{1,0:T(8,128)(2,1)} %constant.25.clone.qih, ...), custom_call_target="tpu_custom_call" | custom-call | tf_op jit(solution)/shard_map/half_transform/pallas_call | solution.py:118
  17.3 27.5 %all_to_all.5 = f32[8,6,32,128]{3,2,1,0:T(8,128)} all-to-all(f32[8,6,32,128]{3,2,1,0:T(8,128)} %half_transform.1), channel_id=1, replica_groups=mesh['wa'=8,'ga'=4] {'wa'}, dimensions={0} | all-to-all | bytes 1572864 | tf_op jit(solution)/shard_map/all_to_all | solution.py:183
  44.8 0.0 all-gather.2.cloned.1.call-update
  44.8 27.7 %all-gather.2.cloned.1.call-done = f32[32,6,32,128]{3,2,1,0:T(8,128)} async-done(((f32[8,6,32,128]{3,2,1,0:T(8,128)}), f32[32,6,32,128]{3,2,1,0:T(8,128)}) %all-gather.2.cloned.1.call-update) | async-done | bytes 3145744 | tf_op jit(solution)/shard_map/all_gather | solution.py:184
  72.5 25.1 %expand.1 = bf16[192,128,128]{2,1,0:T(8,128)(2,1)} custom-call(f32[192,32,128]{2,1,0:T(8,128)} %bitcast.6, bf16[128,512]{1,0:T(8,128)(2,1)} %constant.31.clone.th, bf16[128,512]{1,0:T(8,128)(2,1)} %constant.32.clone.tl), custom_call_target="tpu_custom_call" | custom-call | tf_op jit(solution)/shard_map/expand/pallas_call | solution.py:168
Async XLA Ops:
  6.5 66.0 %all-gather.2.cloned.1.call-start = ((), (), s32[]{:S(2)}) async-start(), calls=%async_computation.1 | async-start | bytes 3932160 | tf_op jit(solution)/shard_map/all_gather | solution.py:184
Sparse Core Ops, SparseCore 0:
  45.0 27.5 all-gather.1
where the time goes:
time: 105 us; the launch traced here: 104 us
  Pallas kernels  35.8 us (34%)
  waiting for transfers between devices  27.7 us (26%)
  blocking collectives  27.5 us (26%)
  between operations  13.4 us (13%)
    all_gather x1, waiting for transfers between devices, regroup(): return lax.all_gather(moved, 'ga', axis=0, tiled=True)  27.7 us
    all_to_all x1, blocking collectives, regroup(): lax.all_to_all(halves, 'wa', split_axis=0, concat_axis=0, tiled=True)  27.5 us
    pallas_call x1, Pallas kernels, expand(): pl.pallas_call(functools.partial(expand_kernel, kept), grid=(total // cou...  25.1 us
    pallas_call x1, Pallas kernels, half_transform(): pl.pallas_call(functools.partial(half_kernel, total), grid_spec=pltpu.Pre...  10.7 us
  transfers between devices with their start and end apart: 1, of which 1 were waited for; matrix products, arithmetic and copies ran while one was open for 0% of the time, Pallas kernels for 0%

commit v1 on v0

--- a/solution.py
+++ b/solution.py
@@ -13,6 +13,8 @@
 S = 32
 RANK = 64
 LANES = 128
+GROUPS = 3
+AXES = ("wa", "ga")
 
 field_width = 0.2
 w_top = 2000.0
@@ -45,21 +47,28 @@
     return v, p.real, p.imag
 
 
+def columns(real, imag):
+    h = RANK // 2
+    return np.concatenate([real[:, :h], imag[:, :h], real[:, h:], imag[:, h:]], 1)
+
+
 def tables(pixels):
     v, pr, pi = factors(pixels)
     zero = np.zeros_like(v)
-    q_re = np_split(np.concatenate([v, zero], 1))
-    q_im = np_split(np.concatenate([zero, v], 1))
+    q_re = np_split(columns(v, zero))
+    q_im = np_split(columns(zero, v))
     vt = np_split(v.T)
     order = np.arange(OS * S).reshape(OS, S // 4, 4).transpose(0, 2, 1).reshape(-1)
     left = np_split(np.concatenate([pr, pi], 1)[order] / pixels)
-    right = np.concatenate(
-        [np.concatenate([pr.T, pi.T], 1), np.concatenate([-pi.T, pr.T], 1)], 0
-    )
+    real, imag = np.concatenate([pr, pi]), np.concatenate([-pi, pr])
+    right = columns(real, imag).T
+    right_hi, right_lo = np_split(right)
+    zeros = np.zeros_like(right_hi[:RANK])
+    low = np.concatenate([right_hi[:RANK], zeros]), np.concatenate([zeros, right_hi[:RANK]])
     coord = (np.arange(pixels) - pixels // 2) / pixels * field_width
     radius = coord[:, None] ** 2 + coord[None, :] ** 2
     nterm = (-radius / (1.0 + np.sqrt(1.0 - radius))).astype(np.float32)
-    return q_re + q_im + vt + left, np_split(right), nterm
+    return q_re + q_im + vt + left, (right_hi, right_lo) + low, nterm
 
 
 def dot3(a, b):
@@ -69,12 +78,11 @@
     return dot(a[0], b[0]) + dot(a[0], b[1]) + dot(a[1], b[0])
 
 
-def half_kernel(
-    total, planes, weight, nterm, qrh, qrl, qih, qil, vth, vtl, lh, ll, out, grh, grl, gih, gil
-):
+def half_plane(wvalue, weight, s, nterm, small, planes, sent):
     pixels = weight.shape[1]
     step = 32
-    wvalue = w_top * planes[pl.program_id(0)].astype(jnp.float32) / total
+    qrh, qrl, qih, qil, vth, vtl, lh, ll = small
+    grh, grl, gih, gil = planes
 
     @pl.loop(0, pixels // step)
     def _(chunk):
@@ -87,16 +95,16 @@
         frac = frac - jnp.round(frac)
         y = math.pi * frac
         z = y * y
-        s = jnp.full_like(z, -1.0 / math.factorial(11))
+        si = jnp.full_like(z, -1.0 / math.factorial(11))
         for k in (9, 7, 5, 3, 1):
-            s = s * z + (-1.0) ** (k // 2) / math.factorial(k)
-        s = s * y
-        c = jnp.full_like(z, 1.0 / math.factorial(12))
+            si = si * z + (-1.0) ** (k // 2) / math.factorial(k)
+        si = si * y
+        co = jnp.full_like(z, 1.0 / math.factorial(12))
         for k in (10, 8, 6, 4, 2, 0):
-            c = c * z + (-1.0) ** (k // 2) / math.factorial(k)
-        w = weight[0, rows, :]
-        g_re = w * (1.0 - 2.0 * s * s)
-        g_im = w * (-2.0 * s * c)
+            co = co * z + (-1.0) ** (k // 2) / math.factorial(k)
+        w = weight[s, rows, :]
+        g_re = w * (1.0 - 2.0 * si * si)
+        g_im = w * (-2.0 * si * co)
         grh[rows, :], grl[rows, :] = split(g_re)
         gih[rows, :], gil[rows, :] = split(g_im)
 
@@ -104,37 +112,171 @@
     t += dot3((gih[...], gil[...]), (qih[...], qil[...]))
     core = dot3((vth[...], vtl[...]), split(t))
     lane = lax.broadcasted_iota(jnp.int32, core.shape, 1)
-    turned = pltpu.roll(core, RANK, 1)
-    turned = jnp.where(lane < RANK, -turned, turned)
-    stacked = jnp.concatenate([core, turned], 0)
-    a = dot3((lh[...], ll[...]), split(stacked))
-    out[...] = a.reshape(out.shape)
-
-
-def half_transform(plane_ids, weighting, total, small, nterm):
+    quarter = RANK // 2
+    turned = jnp.where(
+        lane // quarter % 2 == 0,
+        -pltpu.roll(core, LANES - quarter, 1),
+        pltpu.roll(core, quarter, 1),
+    )
+    a = dot3((lh[...], ll[...]), split(jnp.concatenate([core, turned], 0)))
+    hi = a.astype(jnp.bfloat16)
+    lo = (a - hi.astype(jnp.float32)).reshape(OS, 2, S // 2, LANES)
+    first, second = lo[:, 0].reshape(-1, LANES), lo[:, 1].reshape(-1, LANES)
+    lane = lax.broadcasted_iota(jnp.int32, first.shape, 1)
+    packed = jnp.where(lane < RANK, first, pltpu.roll(second, RANK, 1)).astype(jnp.bfloat16)
+    sent[:, s, 0:S, :] = hi.reshape(OS, S, LANES)
+    sent[:, s, S : S + S // 2, :] = packed.reshape(OS, S // 2, LANES)
+
+
+def exchange_kernel(total, groups, planes_ref, weight, nterm, *refs):
+    small, (held, sent, grh, grl, gih, gil), sems = refs[:8], refs[8:14], refs[14:]
+    ga_count, wa_count, slots = held.shape[:3]
+    per = slots // groups
+    kept = OS * OS // wa_count
+    w_me, g_me = lax.axis_index("wa"), lax.axis_index("ga")
+    g_far = (g_me + 2) % ga_count
+    g_near = g_me + 1 - 2 * (g_me % 2)
+    g_cross = (g_near + 2) % ga_count
+
+    def remote(kind, group, w_block, g_block, w_to, g_to, src=None, slot=None):
+        part = pl.ds(group * per, per)
+        place = held.at[g_block, w_block, part]
+        return pltpu.make_async_remote_copy(
+            src_ref=place if src is None else src,
+            dst_ref=place,
+            send_sem=sems[2 * kind].at[group, w_block if slot is None else slot],
+            recv_sem=sems[2 * kind + 1].at[group, w_block],
+            device_id=(w_to, g_to) if AXES[0] == "wa" else (g_to, w_to),
+            device_id_type=pl.DeviceIdType.MESH,
+        )
+
+    def spread(group, w_to):
+        src = sent.at[w_to * kept // OS, pl.ds(group * per, per)]
+        return remote(0, group, w_me, g_me, w_to, g_me, src, w_to)
+
+    def arrived(group, w_from):
+        return remote(0, group, w_from, g_me, w_from, g_me)
+
+    def far(group, w, g):
+        return remote(1, group, w, g, w_me, g_far)
+
+    def near(group, w, g):
+        return remote(2, group, w, g, w_me, g_near)
+
+    def near_far(group, w, g):
+        return remote(3, group, w, g, w_me, g_near)
+
+    barrier = pltpu.get_barrier_semaphore()
+
+    def greet(w, g):
+        device = (w, g) if AXES[0] == "wa" else (g, w)
+        pl.semaphore_signal(barrier, inc=1, device_id=device, device_id_type=pl.DeviceIdType.MESH)
+
+    @pl.loop(1, wa_count)
+    def _(d):
+        greet((w_me + d) % wa_count, g_me)
+
+    greet(w_me, g_far)
+    greet(w_me, g_near)
+
+    def compute(group):
+        @pl.loop(0, per)
+        def _(i):
+            s = group * per + i
+            wvalue = w_top * planes_ref[s].astype(jnp.float32) / total
+            half_plane(wvalue, weight, s, nterm, small, (grh, grl, gih, gil), sent)
+
+        part = pl.ds(group * per, per)
+        held[g_me, w_me, part] = sent[w_me * kept // OS, part]
+
+    def spread_all(group):
+        @pl.loop(1, wa_count)
+        def _(d):
+            spread(group, (w_me + d) % wa_count).start()
+
+    def forward(group):
+        near(group, w_me, g_me).start()
+        far(group, w_me, g_me).start()
+
+        @pl.loop(1, wa_count)
+        def _(d):
+            w = (w_me + wa_count - d) % wa_count
+            arrived(group, w).wait_recv()
+            far(group, w, g_me).start()
+            near(group, w, g_me).start()
+
+    def forward_far(group):
+        @pl.loop(0, wa_count)
+        def _(d):
+            w = (w_me + wa_count - d) % wa_count
+            far(group, w, g_far).wait_recv()
+            near_far(group, w, g_far).start()
+
+    compute(0)
+    pl.semaphore_wait(barrier, wa_count + 1)
+    spread_all(0)
+
+    @pl.loop(1, groups)
+    def _(group):
+        compute(group)
+        spread_all(group)
+        forward(group - 1)
+
+        @pl.when(group > 1)
+        def _():
+            forward_far(group - 2)
+
+    forward(groups - 1)
+    if groups > 1:
+        forward_far(groups - 2)
+    forward_far(groups - 1)
+
+    @pl.loop(0, groups)
+    def _(group):
+        @pl.loop(1, wa_count)
+        def _(d):
+            spread(group, (w_me + d) % wa_count).wait_send()
+
+        @pl.loop(0, wa_count)
+        def _(w):
+            far(group, w, g_me).wait_send()
+            near(group, w, g_me).wait_send()
+            near_far(group, w, g_far).wait_send()
+            near(group, w, g_near).wait_recv()
+            near_far(group, w, g_cross).wait_recv()
+
+
+def exchange(plane_ids, weighting, total, small, nterm, ga_count, wa_count):
     slots, pixels = weighting.shape[:2]
-    whole = lambda a: pl.BlockSpec(a.shape, lambda s, p: (0,) * a.ndim)
-    args = (nterm,) + small
+    rows = S + S // 2
+    groups = GROUPS if wa_count <= OS and slots % GROUPS == 0 else 1
+    vmem = pl.BlockSpec(memory_space=pltpu.VMEM)
     return pl.pallas_call(
-        functools.partial(half_kernel, total),
-        grid_spec=pltpu.PrefetchScalarGridSpec(
-            num_scalar_prefetch=1,
-            grid=(slots,),
-            in_specs=[pl.BlockSpec((1, pixels, pixels), lambda s, p: (s, 0, 0))]
-            + [whole(a) for a in args],
-            out_specs=pl.BlockSpec((OS, 1, S, LANES), lambda s, p: (0, s, 0, 0)),
-            scratch_shapes=[pltpu.VMEM((pixels, pixels), jnp.bfloat16)] * 4,
-        ),
-        out_shape=jax.ShapeDtypeStruct((OS, slots, S, LANES), jnp.float32),
-        name="half_transform",
-    )(plane_ids, weighting, *args)
-
-
-def expand_kernel(kept, x, th, tl, out, full, mixed):
+        functools.partial(exchange_kernel, total, groups),
+        in_specs=[pl.BlockSpec(memory_space=pltpu.SMEM)] + [vmem] * (2 + len(small)),
+        out_specs=vmem,
+        out_shape=jax.ShapeDtypeStruct((ga_count, wa_count, slots, rows, LANES), jnp.bfloat16),
+        scratch_shapes=[pltpu.VMEM((OS, slots, rows, LANES), jnp.bfloat16)]
+        + [pltpu.VMEM((pixels, pixels), jnp.bfloat16)] * 4
+        + [pltpu.SemaphoreType.DMA((groups, wa_count))] * 8,
+        compiler_params=pltpu.CompilerParams(collective_id=0, has_side_effects=True),
+        name="exchange",
+    )(plane_ids, weighting, nterm, *small)
+
+
+def expand_kernel(kept, x, th, tl, ta, tb, out, full, mixed):
     count = x.shape[0]
     group = 2
-    flat = x[...].reshape(count * S, LANES)
-    full[...] = dot3(split(flat), (th[...], tl[...])).reshape(full.shape)
+    half_rows = S // 2
+
+    def dot(a, b):
+        return jnp.dot(a, b[...], preferred_element_type=jnp.float32)
+
+    hi = x[:, 0:S, :].reshape(count * S, LANES)
+    lo = x[:, S : S + half_rows, :].reshape(count * half_rows, LANES)
+    main = (dot(hi, th) + dot(hi, tl)).reshape(full.shape)
+    full[:, 0:half_rows] = main[:, 0:half_rows] + dot(lo, ta).reshape(count, half_rows, -1)
+    full[:, half_rows:S] = main[:, half_rows:S] + dot(lo, tb).reshape(count, half_rows, -1)
     lane = lax.broadcasted_iota(jnp.int32, (group * 8, LANES), 1) // S
 
     @pl.loop(0, count // group)
@@ -168,7 +310,8 @@
     return pl.pallas_call(
         functools.partial(expand_kernel, kept),
         grid=(total // count,),
-        in_specs=[pl.BlockSpec((count, S, LANES), lambda i: (i, 0, 0))] + [whole(a) for a in right],
+        in_specs=[pl.BlockSpec((count,) + arrived.shape[1:], lambda i: (i, 0, 0))]
+        + [whole(a) for a in right],
         out_specs=pl.BlockSpec((count, 16 * kept, LANES), lambda i: (i, 0, 0)),
         out_shape=jax.ShapeDtypeStruct((total, 16 * kept, LANES), jnp.bfloat16),
         scratch_shapes=[
@@ -179,11 +322,6 @@
     )(arrived, *right)
 
 
-def regroup(halves):
-    moved = lax.all_to_all(halves, "wa", split_axis=0, concat_axis=0, tiled=True)
-    return lax.all_gather(moved, "ga", axis=0, tiled=True)
-
-
 def shards(plane_ids, weighting):
     slots, pixels = weighting.shape[:2]
     wa_count = lax.axis_size("wa")
@@ -191,13 +329,12 @@
     total = slots * wa_count * ga_count
     kept = OS * OS // wa_count
     small, right, nterm = tables(pixels)
-    halves = half_transform(plane_ids, weighting, total, small, nterm)
     if kept < OS:
-        halves = jnp.repeat(halves, OS // kept, axis=0)
         start = lax.axis_index("wa") * kept % OS
         turn = lambda t: jnp.roll(t.reshape(LANES, 2, OS, S), -start, 2).reshape(t.shape)
         right = tuple(turn(jnp.asarray(t)) for t in right)
-    arrived = regroup(halves).reshape(total, S, LANES)
+    arrived = exchange(plane_ids, weighting, total, small, nterm, ga_count, wa_count)
+    arrived = arrived.reshape((total,) + arrived.shape[3:])
     table = expand(arrived, right, kept, 4 * slots)
     table = table.reshape(total, 16, kept, LANES).transpose(0, 2, 1, 3)
     return table.reshape(total, kept, 2 * S * S)

time: 105 us -> 57.7 us (0.55)
  waiting for transfers between devices: 27.7 us -> 0 us
  blocking collectives: 27.5 us -> 0 us
  Pallas kernels: 35.8 us -> 57.5 us
  between operations: 13.4 us -> 0.01 us
    all_gather x1 -> x0, waiting for transfers between devices: 27.7 us -> none  [regroup(): return lax.all_gather(moved, 'ga', axis=0, tiled=True)]
    all_to_all x1 -> x0, blocking collectives: 27.5 us -> none  [regroup(): lax.all_to_all(halves, 'wa', split_axis=0, concat_axis=0, tiled=True)]
    pallas_call x1, Pallas kernels: 10.7 us -> 32.3 us  [exchange(): pl.pallas_call(functools.partial(exchange_kernel, total, groups), in_spec...]
  transfers between devices with their start and end apart: 1 -> 0, of which waited for: 1 -> 0; matrix products, arithmetic and copies ran while one was open for 0% -> 0% of each run, Pallas kernels for 0% -> 0%
where the time goes in v1:
time: 57.7 us; the launch traced here: 57.5 us
  Pallas kernels  57.5 us (100%)
    pallas_call x1, Pallas kernels, exchange(): pl.pallas_call(functools.partial(exchange_kernel, total, groups), in_spec...  32.3 us
    pallas_call x1, Pallas kernels, expand(): pl.pallas_call(functools.partial(expand_kernel, kept), grid=(total // cou...  25.2 us

profile of v1, /device:TPU:0, one launch (start us, length us, event | category | flops | bytes accessed | tf_op | source)
XLA Modules:
  0.0 57.5 jit_solution(17580018031585807626)
XLA Ops:
  0.0 32.3 %exchange.1 = bf16[4,8,6,48,128]{4,3,2,1,0:T(8,128)(2,1)} custom-call(s32[6]{0:T(128)} %planes_ref.1, f32[6,256,256]{2,1,0:T(8,128)} %weight.1, f32[256,256]{1,0:T(8,128)} %constant.26.clone.nterm, bf16[256,128]{1,0:T(8,128)(2,1)} %constant.27.clone.refs_0_, bf16[256,128]{1,0:T(8,128)(2,1)} %constant.28.clone.refs_1_, ...), custom_call_target="tpu_custom_call" | custom-call | tf_op jit(solution)/shard_map/exchange/pallas_call | solution.py:254
  32.4 25.2 %expand.1 = bf16[192,128,128]{2,1,0:T(8,128)(2,1)} custom-call(bf16[192,48,128]{2,1,0:T(8,128)(2,1)} %bitcast.6, bf16[128,512]{1,0:T(8,128)(2,1)} %constant.35.clone.th, bf16[128,512]{1,0:T(8,128)(2,1)} %constant.36.clone.tl, bf16[128,512]{1,0:T(8,128)(2,1)} %constant.37.clone.ta, bf16[128,512]{1,0:T(8,128)(2,1)} %constant.38.clone.tb), custom_call_target="tpu_custom_call" | custom-call | tf_op jit(solution)/shard_map/expand/pallas_call | solution.py:310

commit v2 on v1

--- a/solution.py
+++ b/solution.py
@@ -67,8 +67,11 @@
     low = np.concatenate([right_hi[:RANK], zeros]), np.concatenate([zeros, right_hi[:RANK]])
     coord = (np.arange(pixels) - pixels // 2) / pixels * field_width
     radius = coord[:, None] ** 2 + coord[None, :] ** 2
-    nterm = (-radius / (1.0 + np.sqrt(1.0 - radius))).astype(np.float32)
-    return q_re + q_im + vt + left, (right_hi, right_lo) + low, nterm
+    index = np.arange(pixels) - pixels // 2
+    shift = (index[:, None] + index[None, :]) / (2 * pixels * OS)
+    nterm = np.stack([-radius / (1.0 + np.sqrt(1.0 - radius)), shift]).astype(np.float32)
+    left = left[0], np.concatenate(left, 1)
+    return q_re + q_im + vt + left, (np.concatenate([right_hi, right_lo]),) + low, nterm
 
 
 def dot3(a, b):
@@ -80,7 +83,7 @@
 
 def half_plane(wvalue, weight, s, nterm, small, planes, sent):
     pixels = weight.shape[1]
-    step = 32
+    step = 64
     qrh, qrl, qih, qil, vth, vtl, lh, ll = small
     grh, grl, gih, gil = planes
 
@@ -88,11 +91,8 @@
     def _(chunk):
         start = pl.multiple_of(chunk * step, step)
         rows = pl.ds(start, step)
-        iota = lambda d: lax.broadcasted_iota(jnp.int32, (step, pixels), d)
-        shift = (iota(0) + iota(1) + (start - pixels)).astype(jnp.float32) / (2 * pixels * OS)
-        turns = wvalue * nterm[rows, :]
-        frac = turns - jnp.round(turns) - shift
-        frac = frac - jnp.round(frac)
+        turns = wvalue * nterm[0, rows, :] - nterm[1, rows, :]
+        frac = turns - jnp.round(turns)
         y = math.pi * frac
         z = y * y
         si = jnp.full_like(z, -1.0 / math.factorial(11))
@@ -118,7 +118,9 @@
         -pltpu.roll(core, LANES - quarter, 1),
         pltpu.roll(core, quarter, 1),
     )
-    a = dot3((lh[...], ll[...]), split(jnp.concatenate([core, turned], 0)))
+    xh, xl = split(jnp.concatenate([core, turned], 0))
+    a = jnp.dot(ll[...], jnp.concatenate([xh, xh], 0), preferred_element_type=jnp.float32)
+    a += jnp.dot(lh[...], xl, preferred_element_type=jnp.float32)
     hi = a.astype(jnp.bfloat16)
     lo = (a - hi.astype(jnp.float32)).reshape(OS, 2, S // 2, LANES)
     first, second = lo[:, 0].reshape(-1, LANES), lo[:, 1].reshape(-1, LANES)
@@ -264,9 +266,9 @@
     )(plane_ids, weighting, nterm, *small)
 
 
-def expand_kernel(kept, x, th, tl, ta, tb, out, full, mixed):
+def expand_kernel(kept, x, th, ta, tb, out, full, mixed):
     count = x.shape[0]
-    group = 2
+    group = count // 4
     half_rows = S // 2
 
     def dot(a, b):
@@ -274,7 +276,7 @@
 
     hi = x[:, 0:S, :].reshape(count * S, LANES)
     lo = x[:, S : S + half_rows, :].reshape(count * half_rows, LANES)
-    main = (dot(hi, th) + dot(hi, tl)).reshape(full.shape)
+    main = dot(jnp.concatenate([hi, hi], 1), th).reshape(full.shape)
     full[:, 0:half_rows] = main[:, 0:half_rows] + dot(lo, ta).reshape(count, half_rows, -1)
     full[:, half_rows:S] = main[:, half_rows:S] + dot(lo, tb).reshape(count, half_rows, -1)
     lane = lax.broadcasted_iota(jnp.int32, (group * 8, LANES), 1) // S
@@ -301,6 +303,10 @@
                     if m:
                         y = pltpu.roll(y, LANES - S * m, 1)
                     mixed[slots, comp, pl.ds(kr, 8, stride=kept), :] = y.reshape(group, 8, LANES)
+
+    @pl.loop(0, count // group)
+    def _(i):
+        slots = pl.ds(i * group, group)
         out[slots] = mixed[slots].reshape(group, 16 * kept, LANES).astype(out.dtype)
 
 
@@ -331,7 +337,7 @@
     small, right, nterm = tables(pixels)
     if kept < OS:
         start = lax.axis_index("wa") * kept % OS
-        turn = lambda t: jnp.roll(t.reshape(LANES, 2, OS, S), -start, 2).reshape(t.shape)
+        turn = lambda t: jnp.roll(t.reshape(-1, 2, OS, S), -start, 2).reshape(t.shape)
         right = tuple(turn(jnp.asarray(t)) for t in right)
     arrived = exchange(plane_ids, weighting, total, small, nterm, ga_count, wa_count)
     arrived = arrived.reshape((total,) + arrived.shape[3:])

time: 57.7 us -> 48.1 us (0.83)
  Pallas kernels: 57.5 us -> 47.9 us
    pallas_call x1, Pallas kernels: 25.2 us -> 17.5 us  [expand(): pl.pallas_call(functools.partial(expand_kernel, kept), grid=(total // cou...]
    pallas_call x1, Pallas kernels: 32.3 us -> 30.5 us  [exchange(): pl.pallas_call(functools.partial(exchange_kernel, total, groups), in_spec...]
where the time goes in v2:
time: 48.1 us; the launch traced here: 47.9 us
  Pallas kernels  47.9 us (100%)
    pallas_call x1, Pallas kernels, exchange(): pl.pallas_call(functools.partial(exchange_kernel, total, groups), in_spec...  30.5 us
    pallas_call x1, Pallas kernels, expand(): pl.pallas_call(functools.partial(expand_kernel, kept), grid=(total // cou...  17.5 us

profile of v2, /device:TPU:0, one launch (start us, length us, event | category | flops | bytes accessed | tf_op | source)
XLA Modules:
  0.0 47.9 jit_solution(1731196881020330460)
XLA Ops:
  0.0 30.5 %exchange.1 = bf16[4,8,6,48,128]{4,3,2,1,0:T(8,128)(2,1)} custom-call(s32[6]{0:T(128)} %planes_ref.1, f32[6,256,256]{2,1,0:T(8,128)} %weight.1, f32[2,256,256]{2,1,0:T(8,128)} %constant.24.clone.nterm, bf16[256,128]{1,0:T(8,128)(2,1)} %constant.25.clone.refs_0_, bf16[256,128]{1,0:T(8,128)(2,1)} %constant.26.clone.refs_1_, ...), custom_call_target="tpu_custom_call" | custom-call | tf_op jit(solution)/shard_map/exchange/pallas_call | solution.py:256
  30.5 17.5 %expand.1 = bf16[192,128,128]{2,1,0:T(8,128)(2,1)} custom-call(bf16[192,48,128]{2,1,0:T(8,128)(2,1)} %bitcast.6, bf16[256,512]{1,0:T(8,128)(2,1)} %constant.33.clone.th, bf16[128,512]{1,0:T(8,128)(2,1)} %constant.34.clone.ta, bf16[128,512]{1,0:T(8,128)(2,1)} %constant.35.clone.tb), custom_call_target="tpu_custom_call" | custom-call | tf_op jit(solution)/shard_map/expand/pallas_call | solution.py:316

commit v3 on v2

--- a/solution.py
+++ b/solution.py
@@ -13,7 +13,7 @@
 S = 32
 RANK = 64
 LANES = 128
-GROUPS = 3
+GROUPS = 6
 AXES = ("wa", "ga")
 
 field_width = 0.2
@@ -285,6 +285,7 @@
     def _(i):
         slots = pl.ds(i * group, group)
         for comp in range(2):
+            rows = []
             for half in range(2):
                 tile = comp * 2 + half
                 cols = slice(tile * LANES, (tile + 1) * LANES)
@@ -302,7 +303,17 @@
                         y = jnp.where(lane == b, src[(b - m) % 4], y)
                     if m:
                         y = pltpu.roll(y, LANES - S * m, 1)
-                    mixed[slots, comp, pl.ds(kr, 8, stride=kept), :] = y.reshape(group, 8, LANES)
+                    if kept == OS:
+                        rows.append(y.reshape(group, 8, LANES))
+                    else:
+                        mixed[slots, comp, pl.ds(kr, 8, stride=kept), :] = y.reshape(group, 8, LANES)
+            for k in range(group if kept == OS else 0):
+                tile = jnp.swapaxes(jnp.stack([row[k] for row in rows]), 0, 1)
+                part = pl.ds(comp * 8 * kept, 8 * kept)
+                out[i * group + k, part] = tile.reshape(8 * kept, LANES).astype(out.dtype)
+
+    if kept == OS:
+        return
 
     @pl.loop(0, count // group)
     def _(i):

time: 48.1 us -> 53.8 us (1.12)
  Pallas kernels: 47.9 us -> 53.7 us
    pallas_call x1, Pallas kernels: 30.5 us -> 36.4 us  [exchange(): pl.pallas_call(functools.partial(exchange_kernel, total, groups), in_spec...]
where the time goes in v3:
time: 53.8 us; the launch traced here: 53.7 us
  Pallas kernels  53.7 us (100%)
    pallas_call x1, Pallas kernels, exchange(): pl.pallas_call(functools.partial(exchange_kernel, total, groups), in_spec...  36.4 us
    pallas_call x1, Pallas kernels, expand(): pl.pallas_call(functools.partial(expand_kernel, kept), grid=(total // cou...  17.2 us

profile of v3, /device:TPU:0, one launch (start us, length us, event | category | flops | bytes accessed | tf_op | source)
XLA Modules:
  0.0 53.7 jit_solution(14149423838961645398)
XLA Ops:
  0.0 36.4 %exchange.1 = bf16[4,8,6,48,128]{4,3,2,1,0:T(8,128)(2,1)} custom-call(s32[6]{0:T(128)} %planes_ref.1, f32[6,256,256]{2,1,0:T(8,128)} %weight.1, f32[2,256,256]{2,1,0:T(8,128)} %constant.24.clone.nterm, bf16[256,128]{1,0:T(8,128)(2,1)} %constant.25.clone.refs_0_, bf16[256,128]{1,0:T(8,128)(2,1)} %constant.26.clone.refs_1_, ...), custom_call_target="tpu_custom_call" | custom-call | tf_op jit(solution)/shard_map/exchange/pallas_call | solution.py:256
  36.4 17.2 %expand.1 = bf16[192,128,128]{2,1,0:T(8,128)(2,1)} custom-call(bf16[192,48,128]{2,1,0:T(8,128)(2,1)} %bitcast.6, bf16[256,512]{1,0:T(8,128)(2,1)} %constant.33.clone.th, bf16[128,512]{1,0:T(8,128)(2,1)} %constant.34.clone.ta, bf16[128,512]{1,0:T(8,128)(2,1)} %constant.35.clone.tb), custom_call_target="tpu_custom_call" | custom-call | tf_op jit(solution)/shard_map/expand/pallas_call | solution.py:327

commit v4 on v3

--- a/solution.py
+++ b/solution.py
@@ -13,7 +13,7 @@
 S = 32
 RANK = 64
 LANES = 128
-GROUPS = 6
+GROUPS = 2
 AXES = ("wa", "ga")
 
 field_width = 0.2

time: 53.8 us -> 48.6 us (0.903)
  Pallas kernels: 53.7 us -> 48.3 us
    pallas_call x1, Pallas kernels: 36.4 us -> 31 us  [exchange(): pl.pallas_call(functools.partial(exchange_kernel, total, groups), in_spec...]
where the time goes in v4:
time: 48.6 us; the launch traced here: 48.3 us
  Pallas kernels  48.3 us (99%)
    pallas_call x1, Pallas kernels, exchange(): pl.pallas_call(functools.partial(exchange_kernel, total, groups), in_spec...  31 us
    pallas_call x1, Pallas kernels, expand(): pl.pallas_call(functools.partial(expand_kernel, kept), grid=(total // cou...  17.2 us

profile of v4, /device:TPU:0, one launch (start us, length us, event | category | flops | bytes accessed | tf_op | source)
XLA Modules:
  0.0 48.3 jit_solution(10131673088254459216)
XLA Ops:
  0.0 31.0 %exchange.1 = bf16[4,8,6,48,128]{4,3,2,1,0:T(8,128)(2,1)} custom-call(s32[6]{0:T(128)} %planes_ref.1, f32[6,256,256]{2,1,0:T(8,128)} %weight.1, f32[2,256,256]{2,1,0:T(8,128)} %constant.24.clone.nterm, bf16[256,128]{1,0:T(8,128)(2,1)} %constant.25.clone.refs_0_, bf16[256,128]{1,0:T(8,128)(2,1)} %constant.26.clone.refs_1_, ...), custom_call_target="tpu_custom_call" | custom-call | tf_op jit(solution)/shard_map/exchange/pallas_call | solution.py:256
  31.0 17.2 %expand.1 = bf16[192,128,128]{2,1,0:T(8,128)(2,1)} custom-call(bf16[192,48,128]{2,1,0:T(8,128)(2,1)} %bitcast.6, bf16[256,512]{1,0:T(8,128)(2,1)} %constant.33.clone.th, bf16[128,512]{1,0:T(8,128)(2,1)} %constant.34.clone.ta, bf16[128,512]{1,0:T(8,128)(2,1)} %constant.35.clone.tb), custom_call_target="tpu_custom_call" | custom-call | tf_op jit(solution)/shard_map/expand/pallas_call | solution.py:327
